TPU v7x, 32 devices: a whole 2x2x4 slice. The times are simulated.
32 devices in a mesh: cp: 16 (over z, y, core), tp: 2 (over x).
Axes of the slice: x: 2, y: 2, z: 4, core: 2. Of those that a mesh axis runs over, the one named last changes fastest.
Arguments:
- hidden_in: bfloat16 [4096, 5120], P('cp', 'tp'), may hold values from -6 to 6
- norm_gain: float32 [5120], replicated, may hold values from 0.25 to 1.75
- seq_lengths: int32 [16], replicated, may hold values from 1 to 3072, 4096 in all
- w_query: bfloat16 [5120, 3072], P(None, 'tp'), may hold values from -0.078125 to 0.078125
- b_query: bfloat16 [3072], P('tp'), may hold values from -400 to 400
- w_key: bfloat16 [5120, 1024], P(None, 'tp'), may hold values from -0.078125 to 0.078125
- b_key: bfloat16 [1024], P('tp'), may hold values from -3 to 3
- w_value: bfloat16 [5120, 1024], P(None, 'tp'), may hold values from -0.078125 to 0.078125
- b_value: bfloat16 [1024], P('tp'), may hold values from -3 to 3
- w_out: bfloat16 [3072, 5120], P(None, 'tp'), may hold values from -0.109375 to 0.109375
Outputs:
- mixed: bfloat16 [4096, 5120], P('cp', 'tp')
- k_cache: bfloat16 [4096, 1024], P('cp', 'tp')
- v_cache: bfloat16 [4096, 1024], P('cp', 'tp')
Inputs may be any that keep to these rules, and one draw needn't show every extreme that they name: `seq_lengths`: they sum to 4096; the longest is exactly 3072.
All inputs are finite; a program needn't handle non-finite values.
Results may differ from a plain program's by a relative error of at most 0.012.
The roundings to bfloat16 on the way count: a program that leaves them out, or rounds other values in their place, can miss the bound.
Values may be sent and summed in bfloat16 or wider, within the bound.
No kernel may reach another device: no remote copies, remote signals or barrier semaphores. Data moves between devices by JAX's collectives and lax.ppermute only.
A program may use at most 128 MiB of HBM per device.

v0:
```python
import jax
import jax.numpy as jnp
from jax import lax
from jax.sharding import PartitionSpec as P

HD = 128


EPS = 1e-06
ROPE_BASE = 1000000.0
NEG = -1e30


def doc_tables(seq_lengths, positions):
    ends = jnp.cumsum(seq_lengths)
    starts = ends - seq_lengths
    after = positions[:, None] >= ends[None, :]
    docs = jnp.sum(after.astype(jnp.int32), axis=1)
    inside = (positions[:, None] >= starts[None, :]) & jnp.logical_not(after)
    offset = jnp.sum(jnp.where(inside, starts[None, :], 0), axis=1)
    return (docs, positions - offset)


def rotate(values, positions):
    half = values.shape[-1] // 2
    freq = ROPE_BASE ** (-jnp.arange(half, dtype=jnp.float32) / half)
    angle = positions.astype(jnp.float32)[:, None] * freq[None, :]
    cosine = jnp.cos(angle)[:, None, :]
    sine = jnp.sin(angle)[:, None, :]
    first = values[..., :half]
    second = values[..., half:]
    return jnp.concatenate(
        [first * cosine - second * sine, second * cosine + first * sine], axis=-1
    )


def local(
    hidden_in, norm_gain, seq_lengths, w_query, b_query, w_key, b_key, w_value, b_value, w_out
):
    tok_rows = hidden_in.shape[0]
    gathered = lax.all_gather(hidden_in, "tp", axis=1, tiled=True)
    widened = gathered.astype(jnp.float32)
    normed = (
        widened * lax.rsqrt(jnp.mean(widened * widened, axis=-1, keepdims=True) + EPS) * norm_gain
    ).astype(jnp.bfloat16)
    cp_index = lax.axis_index("cp")
    positions = cp_index * tok_rows + jnp.arange(tok_rows, dtype=jnp.int32)
    docs, local_pos = doc_tables(seq_lengths, positions)
    query = jnp.dot(normed, w_query, preferred_element_type=jnp.float32) + b_query.astype(
        jnp.float32
    )
    query = rotate(query.reshape(tok_rows, -1, HD), local_pos).astype(jnp.bfloat16)
    key_heads = jnp.dot(normed, w_key, preferred_element_type=jnp.float32) + b_key.astype(
        jnp.float32
    )
    key_heads = rotate(key_heads.reshape(tok_rows, -1, HD), local_pos).astype(jnp.bfloat16)
    value_flat = (
        jnp.dot(normed, w_value, preferred_element_type=jnp.float32) + b_value.astype(jnp.float32)
    ).astype(jnp.bfloat16)
    kv_heads = key_heads.shape[1]
    value_heads = value_flat.reshape(tok_rows, kv_heads, HD)
    group = query.shape[1] // kv_heads
    grouped = query.reshape(tok_rows, kv_heads, group, HD)
    scale = HD ** (-0.5)

    def update(carried, key_block, value_block, start):
        count = key_block.shape[0]
        key_pos = start + jnp.arange(count, dtype=jnp.int32)
        key_docs, unused_pos = doc_tables(seq_lengths, key_pos)
        allowed = (
            (key_pos[None, :] <= positions[:, None])
            & (key_docs[None, :] == docs[:, None])
            & (key_pos[None, :] >= 0)
        )

        def compute(state):
            running, totals, accum = state
            scores = (
                jnp.einsum("qhgd,khd->hgqk", grouped, key_block, preferred_element_type=jnp.float32)
                * scale
            )
            highest = jnp.max(jnp.where(allowed, scores, NEG), axis=-1)
            fresh = jnp.maximum(running, highest)
            weights = jnp.exp(jnp.where(allowed, scores - fresh[..., None], NEG))
            factor = jnp.exp(running - fresh)
            totals = totals * factor + jnp.sum(weights, axis=-1)
            added = jnp.einsum(
                "hgqk,khd->qhgd",
                weights.astype(jnp.bfloat16),
                value_block,
                preferred_element_type=jnp.float32,
            )
            accum = accum * jnp.transpose(factor, (2, 0, 1))[..., None] + added
            return (fresh, totals, accum)

        def unchanged(state):
            return state

        return lax.cond(jnp.any(allowed), compute, unchanged, carried)

    initial = (
        jnp.full((kv_heads, group, tok_rows), NEG, jnp.float32),
        jnp.zeros((kv_heads, group, tok_rows), jnp.float32),
        jnp.zeros((tok_rows, kv_heads, group, HD), jnp.float32),
    )
    carried = initial
    key_rows = lax.all_gather(key_heads, "cp", axis=0, tiled=True)
    count = key_rows.shape[0]
    width = 512
    blocks = count // width
    key_split = key_rows.reshape(blocks, width, kv_heads, HD)
    value_split = lax.all_gather(value_heads, "cp", axis=0, tiled=True).reshape(
        blocks, width, kv_heads, HD
    )

    def advance(state, items):
        return (update(state, items[0], items[1], items[2] * width), None)

    carried, unused_out = lax.scan(
        advance, carried, (key_split, value_split, jnp.arange(blocks, dtype=jnp.int32))
    )
    running, totals, accum = carried
    attended = (
        (accum / jnp.transpose(totals, (2, 0, 1))[..., None])
        .astype(jnp.bfloat16)
        .reshape(tok_rows, -1)
    )
    summed = jnp.dot(
        lax.all_gather(attended, "tp", axis=1, tiled=True),
        w_out,
        preferred_element_type=jnp.float32,
    )
    mixed = (hidden_in.astype(jnp.float32) + summed).astype(jnp.bfloat16)
    return (mixed, key_heads.reshape(tok_rows, -1), value_flat)


def solution(mesh):
    placed = (
        P("cp", "tp"),
        P(),
        P(),
        P(None, "tp"),
        P("tp"),
        P(None, "tp"),
        P("tp"),
        P(None, "tp"),
        P("tp"),
        P(None, "tp"),
    )
    return jax.shard_map(
        local,
        mesh=mesh,
        in_specs=placed,
        out_specs=(P("cp", "tp"), P("cp", "tp"), P("cp", "tp")),
        check_vma=False,
    )
```

profile of v0, /device:TPU:25, one launch (start us, length us, event | category | flops | bytes accessed | tf_op | source)
XLA Modules:
  0.0 286.0 jit_solution(7243798167090336275)
XLA Ops:
  10.8 38.5 %all-gather.5.cloned.1.call-done = bf16[256,5120]{1,0:T(8,128)(2,1)} async-done(((bf16[256,2560]{1,0:T(8,128)(2,1)}), bf16[256,5120]{1,0:T(8,128)(2,1)}) %all-gather.5.cloned.1.call-update) | async-done | bytes 2621456 | tf_op jit(solution)/shard_map/all_gather | solution.py:41
  49.4 2.3 fusion.25
  51.7 5.7 %convolution_add_fusion.3 = f32[256,512]{1,0:T(8,128)} fusion(bf16[5120,512]{1,0:T(8,128)(2,1)} %param.19, f32[512]{0:T(512)S(1)} %convert_element_type.66, bf16[256,5120]{1,0:T(8,128)(2,1)} %all-gather.5.cloned.1.call-done, f32[5120]{0:T(1024)S(1)} %copy-done.7, f32[256]{0:T(256)S(1)} %add_rsqrt_fusion), kind=kOutput, calls=%fused_computation.41 | convolution fusion | flops 1347551232 | bytes 8412160 | tf_op jit(solution)/shard_map/dot_general | solution.py:53
  57.4 1.4 reshape.163
  60.2 4.1 %fusion.29 = bf16[256,512]{1,0:T(8,128)(2,1)S(1)} fusion(bf16[5120,512]{1,0:T(8,128)(2,1)} %param.21, f32[512]{0:T(512)S(1)} %convert_element_type.70, bf16[256,5120]{1,0:T(8,128)(2,1)S(1)} %copy-done.1, f32[5120]{0:T(1024)} %param.15, f32[256]{0:T(256)S(1)} %add_rsqrt_fusion), kind=kOutput, calls=%fused_computation.42 | convolution fusion | flops 1347682304 | bytes 8150016 | tf_op jit(solution)/shard_map/dot_general | solution.py:58
  65.6 9.3 %convolution_add_fusion.1 = f32[256,1536]{1,0:T(8,128)} fusion(bf16[5120,1536]{1,0:T(8,128)(2,1)} %param.17, f32[1536]{0:T(1024)S(1)} %convert_element_type.69, bf16[256,5120]{1,0:T(8,128)(2,1)S(1)} %copy-done.1, f32[5120]{0:T(1024)S(1)} %copy-done.8, f32[256]{0:T(256)S(1)} %add_rsqrt_fusion), kind=kOutput, calls=%fused_computation.38 | convolution fusion | flops 4032167936 | bytes 19950592 | tf_op jit(solution)/shard_map/dot_general | solution.py:49
  74.8 1.9 copy.66
  78.2 31.6 %all-gather.7.cloned.1.call-done = bf16[4096,4,128]{2,0,1:T(8,128)(2,1)} async-done(((bf16[256,4,128]{2,0,1:T(8,128)(2,1)}), bf16[4096,4,128]{2,0,1:T(8,128)(2,1)}) %all-gather.7.cloned.1.call-update) | async-done | bytes 4194320 | tf_op jit(solution)/shard_map/all_gather | solution.py:107
  109.8 4.6 %copy.70 = bf16[8,512,4,128]{3,1,2,0:T(8,128)(2,1)} copy(bf16[8,512,4,128]{3,1,0,2:T(8,128)(2,1)} %bitcast.62) | data formatting | bytes 8388608
  114.3 47.1 %all-gather.9.cloned.1.call-done = bf16[4096,4,128]{2,0,1:T(8,128)(2,1)} async-done(((bf16[256,4,128]{2,0,1:T(8,128)(2,1)}), bf16[4096,4,128]{2,0,1:T(8,128)(2,1)}) %all-gather.9.cloned.1.call-update) | async-done | bytes 4194320 | tf_op jit(solution)/shard_map/all_gather | solution.py:112
  161.5 4.6 %copy.71 = bf16[8,512,4,128]{3,1,2,0:T(8,128)(2,1)} copy(bf16[8,512,4,128]{3,1,0,2:T(8,128)(2,1)} %bitcast.63) | data formatting | bytes 8388608
  166.3 64.2 %while.17 = (s32[]{:T(128)}, f32[4,3,256]{2,1,0:T(4,128)S(1)}, f32[4,3,256]{2,1,0:T(4,128)S(1)}, f32[256,4,3,128]{3,0,2,1:T(8,128)S(1)}, s32[8]{0:T(128)S(1)}, /...) while((s32[]{:T(128)}, f32[4,3,256]{2,1,0:T(4,128)S(1)}, ...), condition=%wide.region_12.13_spmd.clone, body=%wide.region_5.12_spmd.clone.sunk | while | flops 824084736 | bytes 24591712 | solution.py:119
  167.6 0.9 fusion.45
  170.6 0.9 fusion.45
  172.1 6.8 %conditional.3 = ((f32[4,3,256]{2,1,0:T(4,128)S(1)}, f32[4,3,256]{2,1,0:T(4,128)S(1)}, f32[256,4,3,128]{3,0,2,1:T(8,128)S(1)})) conditional(s32[]{:T(128)} %convert_element_type.109, (f32[4,3,256]{2,1,0:T(4,128)S(1)}, f32[4,3,256]{2,1,0:T(4,128)S(1)}, f32[256,4,3,128]{3,0,2,1:T(8,128)S(1)}) %tuple.65, (pred[256,512]{0,1:T(8,128)(4,1)S(1)}, ...), branch_computations={%region_8.8_spmd, %region_9.11_spmd} | conditional | flops 823403520 | bytes 24445984 | solution.py:99
  172.2 2.1 fusion.2
  174.3 3.3 %bitcast_add_fusion = f32[256,4,3,128]{3,0,2,1:T(8,128)S(1)} fusion(f32[256,4,3,128]{3,0,2,1:T(8,128)S(1)} %get-tuple-element.188, f32[4,512,256,3]{2,1,3,0:T(8,128)S(1)} %get-tuple-element.322, f32[4,3,256]{2,1,0:T(4,128)S(1)} %get-tuple-element.411, pred[256,512]{0,1:T(8,128)(4,1)S(1)} %get-tuple-element.183, f32[256,4,3]{0,2,1:T(4,128)S(1)} %get-tuple-element.317, ...), kind=kOutput, calls=%fused_computation.13 | convolution fusion | flops 409731072 | bytes 10117632 | tf_op jit(solution)/shard_map/while/body/eval_jaxpr/cond/branch_1_fun/hgqk,khd->qhgd/dot_general | solution.py:87
  177.6 1.3 fusion.6
  180.3 0.9 fusion.45
  181.9 6.8 %conditional.3 = ((f32[4,3,256]{2,1,0:T(4,128)S(1)}, f32[4,3,256]{2,1,0:T(4,128)S(1)}, f32[256,4,3,128]{3,0,2,1:T(8,128)S(1)})) conditional(s32[]{:T(128)} %convert_element_type.109, (f32[4,3,256]{2,1,0:T(4,128)S(1)}, f32[4,3,256]{2,1,0:T(4,128)S(1)}, f32[256,4,3,128]{3,0,2,1:T(8,128)S(1)}) %tuple.65, (pred[256,512]{0,1:T(8,128)(4,1)S(1)}, ...), branch_computations={%region_8.8_spmd, %region_9.11_spmd} | conditional | flops 823403520 | bytes 24445984 | solution.py:99
  181.9 2.1 fusion.2
  184.0 3.3 %bitcast_add_fusion = f32[256,4,3,128]{3,0,2,1:T(8,128)S(1)} fusion(f32[256,4,3,128]{3,0,2,1:T(8,128)S(1)} %get-tuple-element.188, f32[4,512,256,3]{2,1,3,0:T(8,128)S(1)} %get-tuple-element.322, f32[4,3,256]{2,1,0:T(4,128)S(1)} %get-tuple-element.411, pred[256,512]{0,1:T(8,128)(4,1)S(1)} %get-tuple-element.183, f32[256,4,3]{0,2,1:T(4,128)S(1)} %get-tuple-element.317, ...), kind=kOutput, calls=%fused_computation.13 | convolution fusion | flops 409731072 | bytes 10117632 | tf_op jit(solution)/shard_map/while/body/eval_jaxpr/cond/branch_1_fun/hgqk,khd->qhgd/dot_general | solution.py:87
  187.3 1.3 fusion.6
  190.0 0.9 fusion.45
  191.6 6.8 %conditional.3 = ((f32[4,3,256]{2,1,0:T(4,128)S(1)}, f32[4,3,256]{2,1,0:T(4,128)S(1)}, f32[256,4,3,128]{3,0,2,1:T(8,128)S(1)})) conditional(s32[]{:T(128)} %convert_element_type.109, (f32[4,3,256]{2,1,0:T(4,128)S(1)}, f32[4,3,256]{2,1,0:T(4,128)S(1)}, f32[256,4,3,128]{3,0,2,1:T(8,128)S(1)}) %tuple.65, (pred[256,512]{0,1:T(8,128)(4,1)S(1)}, ...), branch_computations={%region_8.8_spmd, %region_9.11_spmd} | conditional | flops 823403520 | bytes 24445984 | solution.py:99
  191.6 2.1 fusion.2
  193.7 3.3 %bitcast_add_fusion = f32[256,4,3,128]{3,0,2,1:T(8,128)S(1)} fusion(f32[256,4,3,128]{3,0,2,1:T(8,128)S(1)} %get-tuple-element.188, f32[4,512,256,3]{2,1,3,0:T(8,128)S(1)} %get-tuple-element.322, f32[4,3,256]{2,1,0:T(4,128)S(1)} %get-tuple-element.411, pred[256,512]{0,1:T(8,128)(4,1)S(1)} %get-tuple-element.183, f32[256,4,3]{0,2,1:T(4,128)S(1)} %get-tuple-element.317, ...), kind=kOutput, calls=%fused_computation.13 | convolution fusion | flops 409731072 | bytes 10117632 | tf_op jit(solution)/shard_map/while/body/eval_jaxpr/cond/branch_1_fun/hgqk,khd->qhgd/dot_general | solution.py:87
  197.0 1.3 fusion.6
  199.7 0.9 fusion.45
  201.3 6.8 %conditional.3 = ((f32[4,3,256]{2,1,0:T(4,128)S(1)}, f32[4,3,256]{2,1,0:T(4,128)S(1)}, f32[256,4,3,128]{3,0,2,1:T(8,128)S(1)})) conditional(s32[]{:T(128)} %convert_element_type.109, (f32[4,3,256]{2,1,0:T(4,128)S(1)}, f32[4,3,256]{2,1,0:T(4,128)S(1)}, f32[256,4,3,128]{3,0,2,1:T(8,128)S(1)}) %tuple.65, (pred[256,512]{0,1:T(8,128)(4,1)S(1)}, ...), branch_computations={%region_8.8_spmd, %region_9.11_spmd} | conditional | flops 823403520 | bytes 24445984 | solution.py:99
  201.3 2.1 fusion.2
  203.5 3.3 %bitcast_add_fusion = f32[256,4,3,128]{3,0,2,1:T(8,128)S(1)} fusion(f32[256,4,3,128]{3,0,2,1:T(8,128)S(1)} %get-tuple-element.188, f32[4,512,256,3]{2,1,3,0:T(8,128)S(1)} %get-tuple-element.322, f32[4,3,256]{2,1,0:T(4,128)S(1)} %get-tuple-element.411, pred[256,512]{0,1:T(8,128)(4,1)S(1)} %get-tuple-element.183, f32[256,4,3]{0,2,1:T(4,128)S(1)} %get-tuple-element.317, ...), kind=kOutput, calls=%fused_computation.13 | convolution fusion | flops 409731072 | bytes 10117632 | tf_op jit(solution)/shard_map/while/body/eval_jaxpr/cond/branch_1_fun/hgqk,khd->qhgd/dot_general | solution.py:87
  206.7 1.3 fusion.6
  209.4 0.9 fusion.45
  211.0 6.8 %conditional.3 = ((f32[4,3,256]{2,1,0:T(4,128)S(1)}, f32[4,3,256]{2,1,0:T(4,128)S(1)}, f32[256,4,3,128]{3,0,2,1:T(8,128)S(1)})) conditional(s32[]{:T(128)} %convert_element_type.109, (f32[4,3,256]{2,1,0:T(4,128)S(1)}, f32[4,3,256]{2,1,0:T(4,128)S(1)}, f32[256,4,3,128]{3,0,2,1:T(8,128)S(1)}) %tuple.65, (pred[256,512]{0,1:T(8,128)(4,1)S(1)}, ...), branch_computations={%region_8.8_spmd, %region_9.11_spmd} | conditional | flops 823403520 | bytes 24445984 | solution.py:99
  211.0 2.1 fusion.2
  213.2 3.3 %bitcast_add_fusion = f32[256,4,3,128]{3,0,2,1:T(8,128)S(1)} fusion(f32[256,4,3,128]{3,0,2,1:T(8,128)S(1)} %get-tuple-element.188, f32[4,512,256,3]{2,1,3,0:T(8,128)S(1)} %get-tuple-element.322, f32[4,3,256]{2,1,0:T(4,128)S(1)} %get-tuple-element.411, pred[256,512]{0,1:T(8,128)(4,1)S(1)} %get-tuple-element.183, f32[256,4,3]{0,2,1:T(4,128)S(1)} %get-tuple-element.317, ...), kind=kOutput, calls=%fused_computation.13 | convolution fusion | flops 409731072 | bytes 10117632 | tf_op jit(solution)/shard_map/while/body/eval_jaxpr/cond/branch_1_fun/hgqk,khd->qhgd/dot_general | solution.py:87
  216.5 1.3 fusion.6
  219.2 0.9 fusion.45
  220.7 6.8 %conditional.3 = ((f32[4,3,256]{2,1,0:T(4,128)S(1)}, f32[4,3,256]{2,1,0:T(4,128)S(1)}, f32[256,4,3,128]{3,0,2,1:T(8,128)S(1)})) conditional(s32[]{:T(128)} %convert_element_type.109, (f32[4,3,256]{2,1,0:T(4,128)S(1)}, f32[4,3,256]{2,1,0:T(4,128)S(1)}, f32[256,4,3,128]{3,0,2,1:T(8,128)S(1)}) %tuple.65, (pred[256,512]{0,1:T(8,128)(4,1)S(1)}, ...), branch_computations={%region_8.8_spmd, %region_9.11_spmd} | conditional | flops 823403520 | bytes 24445984 | solution.py:99
  220.7 2.1 fusion.2
  222.9 3.3 %bitcast_add_fusion = f32[256,4,3,128]{3,0,2,1:T(8,128)S(1)} fusion(f32[256,4,3,128]{3,0,2,1:T(8,128)S(1)} %get-tuple-element.188, f32[4,512,256,3]{2,1,3,0:T(8,128)S(1)} %get-tuple-element.322, f32[4,3,256]{2,1,0:T(4,128)S(1)} %get-tuple-element.411, pred[256,512]{0,1:T(8,128)(4,1)S(1)} %get-tuple-element.183, f32[256,4,3]{0,2,1:T(4,128)S(1)} %get-tuple-element.317, ...), kind=kOutput, calls=%fused_computation.13 | convolution fusion | flops 409731072 | bytes 10117632 | tf_op jit(solution)/shard_map/while/body/eval_jaxpr/cond/branch_1_fun/hgqk,khd->qhgd/dot_general | solution.py:87
  226.2 1.3 fusion.6
  228.9 0.9 fusion.45
  230.5 1.6 copy.72
  232.1 2.5 divide_convert_fusion
  235.7 32.5 %all-gather.11.cloned.1.call-done = bf16[256,3072]{0,1:T(8,128)(2,1)} async-done(((bf16[256,1536]{0,1:T(8,128)(2,1)}), bf16[256,3072]{0,1:T(8,128)(2,1)}) %all-gather.11.cloned.1.call-update) | async-done | bytes 1572880 | tf_op jit(solution)/shard_map/all_gather | solution.py:129
  268.2 11.3 %fusion.28 = bf16[256,2560]{1,0:T(8,128)(2,1)} fusion(bf16[256,3072]{0,1:T(8,128)(2,1)} %all-gather.11.cloned.1.call-done, bf16[3072,2560]{1,0:T(8,128)(2,1)} %param.23, bf16[256,2560]{1,0:T(8,128)(2,1)S(1)} %copy-done), kind=kOutput, calls=%fused_computation.37 | convolution fusion | flops 4028497920 | bytes 19922944 | tf_op jit(solution)/shard_map/dot_general | solution.py:128
  (116 shorter events, 14.6 us)
Async XLA Ops:
  7.2 44.6 %copy-start.7 = (f32[5120]{0:T(1024)S(1)}, f32[5120]{0:T(1024)}, u32[]{:S(2)}) copy-start(f32[5120]{0:T(1024)} %param.15) | copy-start | bytes 61444
  7.2 42.2 %all-gather.5.cloned.1.call-start = ((), (), s32[]{:S(2)}) async-start(), calls=%async_computation | async-start | bytes 3932160 | tf_op jit(solution)/shard_map/all_gather | solution.py:41
  7.9 101.9 %all-gather.7.cloned.1.call-start = ((), (), s32[]{:S(2)}) async-start(), calls=%async_computation.1 | async-start | bytes 4456448 | tf_op jit(solution)/shard_map/all_gather | solution.py:107
  57.4 2.8 copy-start.5
  57.4 2.8 copy-start.1
  60.1 101.4 %all-gather.9.cloned.1.call-start = ((), (), s32[]{:S(2)}) async-start(), calls=%async_computation.2 | async-start | bytes 4456448 | tf_op jit(solution)/shard_map/all_gather | solution.py:112
  60.2 5.2 %copy-start.4 = (bf16[1536]{0:T(1024)(128)(2,1)S(1)}, bf16[1536]{0:T(1024)(128)(2,1)}, u32[]{:S(2)}) copy-start(bf16[1536]{0:T(1024)(128)(2,1)} %param.18) | copy-start | bytes 9220
  60.2 5.2 %copy-start.6 = (s32[16]{0:T(128)S(1)}, s32[16]{0:T(128)}, u32[]{:S(2)}) copy-start(s32[16]{0:T(128)} %param.16) | copy-start | bytes 196
  60.2 5.4 %copy-start.8 = (f32[5120]{0:T(1024)S(1)}, f32[5120]{0:T(1024)}, u32[]{:S(2)}) copy-start(f32[5120]{0:T(1024)} %param.15) | copy-start | bytes 61444
  64.3 10.5 %copy-start.3 = (bf16[256,512]{1,0:T(8,128)(2,1)}, bf16[256,512]{1,0:T(8,128)(2,1)S(1)}, u32[]{:S(2)}) copy-start(bf16[256,512]{1,0:T(8,128)(2,1)S(1)} %fusion.29) | copy-start | bytes 786436
  65.1 203.1 %all-gather.11.cloned.1.call-start = ((), (), s32[]{:S(2)}) async-start(), calls=%async_computation.3 | async-start | bytes 2359296 | tf_op jit(solution)/shard_map/all_gather | solution.py:129
  230.5 4.2 %copy-start.2 = (bf16[256,4,128]{2,0,1:T(8,128)(2,1)S(1)}, bf16[256,4,128]{2,0,1:T(8,128)(2,1)}, u32[]{:S(2)}) copy-start(bf16[256,4,128]{2,0,1:T(8,128)(2,1)} %maximum_convert_fusion) | copy-start | bytes 786436
  232.1 36.1 %copy-start = (bf16[256,2560]{1,0:T(8,128)(2,1)S(1)}, bf16[256,2560]{1,0:T(8,128)(2,1)}, u32[]{:S(2)}) copy-start(bf16[256,2560]{1,0:T(8,128)(2,1)} %param.14) | copy-start | bytes 3932164
Sparse Core Ops, SparseCore 0:
  9.5 39.7 all-gather.4
  60.2 49.4 all-gather.6
  112.5 48.9 all-gather.8
  234.8 33.3 all-gather.10
where the time goes:
time: 289 us; the launch traced here: 286 us
  waiting for transfers between devices  151 us (52%)
  matrix products  62.7 us (22%)
  other arithmetic  24.7 us (9%)
  local copies, waits for them, and re-layouts  22.8 us (8%)
  between operations  14 us (5%)
  loops' own time  11.1 us (4%)
    all_gather x1, waiting for transfers between devices, local(): lax.all_gather(value_heads, 'cp', axis=0, tiled=True)  47.1 us
    all_gather x1, waiting for transfers between devices, local(): gathered = lax.all_gather(hidden_in, 'tp', axis=1, tiled=True)  38.5 us
    all_gather x1, waiting for transfers between devices, local(): lax.all_gather(attended, 'tp', axis=1, tiled=True)  32.5 us
    all_gather x1, waiting for transfers between devices, local(): key_rows = lax.all_gather(key_heads, 'cp', axis=0, tiled=True)  31.6 us
    dot_general x6, matrix products, compute(): jnp.einsum('hgqk,khd->qhgd', weights.astype(jnp.bfloat16), value_block, p...  19.7 us
    dot_general x6, matrix products, compute(): jnp.einsum('qhgd,khd->hgqk', grouped, key_block, preferred_element_type=j...  12.7 us
    dot_general x1, matrix products, local(): jnp.dot(lax.all_gather(attended, 'tp', axis=1, tiled=True), w_out, prefer...  11.3 us
    another operation x1, loops' own time, local(): lax.scan(advance, carried, (key_split, value_split, jnp.arange(blocks, dt...  10.7 us
  transfers between devices with their start and end apart: 4, of which 4 were waited for; matrix products, arithmetic and copies ran while one was open for 9% of the time, Pallas kernels for 0%

commit v1 on v0

--- a/solution.py
+++ b/solution.py
@@ -1,14 +1,19 @@
+import functools
+import math
+
 import jax
 import jax.numpy as jnp
 from jax import lax
+from jax.experimental import pallas as pl
+from jax.experimental.pallas import tpu as pltpu
 from jax.sharding import PartitionSpec as P
 
 HD = 128
-
-
 EPS = 1e-06
 ROPE_BASE = 1000000.0
 NEG = -1e30
+CHUNKS = 2
+SIZES = ("cp", "tp")
 
 
 def doc_tables(seq_lengths, positions):
@@ -34,7 +39,7 @@
     )
 
 
-def local(
+def general(
     hidden_in, norm_gain, seq_lengths, w_query, b_query, w_key, b_key, w_value, b_value, w_out
 ):
     tok_rows = hidden_in.shape[0]
@@ -67,11 +72,7 @@
         count = key_block.shape[0]
         key_pos = start + jnp.arange(count, dtype=jnp.int32)
         key_docs, unused_pos = doc_tables(seq_lengths, key_pos)
-        allowed = (
-            (key_pos[None, :] <= positions[:, None])
-            & (key_docs[None, :] == docs[:, None])
-            & (key_pos[None, :] >= 0)
-        )
+        allowed = (key_pos[None, :] <= positions[:, None]) & (key_docs[None, :] == docs[:, None])
 
         def compute(state):
             running, totals, accum = state
@@ -81,7 +82,7 @@
             )
             highest = jnp.max(jnp.where(allowed, scores, NEG), axis=-1)
             fresh = jnp.maximum(running, highest)
-            weights = jnp.exp(jnp.where(allowed, scores - fresh[..., None], NEG))
+            weights = jnp.where(allowed, jnp.exp(scores - fresh[..., None]), 0.0)
             factor = jnp.exp(running - fresh)
             totals = totals * factor + jnp.sum(weights, axis=-1)
             added = jnp.einsum(
@@ -93,20 +94,16 @@
             accum = accum * jnp.transpose(factor, (2, 0, 1))[..., None] + added
             return (fresh, totals, accum)
 
-        def unchanged(state):
-            return state
-
-        return lax.cond(jnp.any(allowed), compute, unchanged, carried)
-
-    initial = (
+        return lax.cond(jnp.any(allowed), compute, lambda state: state, carried)
+
+    carried = (
         jnp.full((kv_heads, group, tok_rows), NEG, jnp.float32),
         jnp.zeros((kv_heads, group, tok_rows), jnp.float32),
         jnp.zeros((tok_rows, kv_heads, group, HD), jnp.float32),
     )
-    carried = initial
     key_rows = lax.all_gather(key_heads, "cp", axis=0, tiled=True)
     count = key_rows.shape[0]
-    width = 512
+    width = math.gcd(512, count)
     blocks = count // width
     key_split = key_rows.reshape(blocks, width, kv_heads, HD)
     value_split = lax.all_gather(value_heads, "cp", axis=0, tiled=True).reshape(
@@ -132,6 +129,419 @@
     )
     mixed = (hidden_in.astype(jnp.float32) + summed).astype(jnp.bfloat16)
     return (mixed, key_heads.reshape(tok_rows, -1), value_flat)
+
+
+def turned(u, cosf, sinf):
+    return u * cosf + pltpu.roll(u, HD // 2, 1) * sinf
+
+
+def kv_kernel(s_ref, own_ref, got_ref, gain_ref, cos_ref, sin_ref, wk_ref, wv_ref, bk_ref, bv_ref,
+              k_ref, v_ref, keep_ref, send_ref, normed_ref):
+    tp = s_ref[0]
+    half = own_ref.shape[1]
+    j = pl.program_id(0)
+
+    @pl.when(j == 0)
+    def _():
+        own = own_ref[...].astype(jnp.float32)
+        got = got_ref[...].astype(jnp.float32)
+        total = jnp.sum(own * own, axis=1, keepdims=True) + jnp.sum(got * got, axis=1, keepdims=True)
+        factor = lax.rsqrt(total / (2 * half) + EPS)
+        here = pl.ds(pl.multiple_of(tp * half, half), half)
+        there = pl.ds(pl.multiple_of((1 - tp) * half, half), half)
+        normed_ref[:, here] = (own * factor * gain_ref[:, here]).astype(jnp.bfloat16)
+        normed_ref[:, there] = (got * factor * gain_ref[:, there]).astype(jnp.bfloat16)
+
+    x = normed_ref[...]
+    keys = jnp.dot(x, wk_ref[...], preferred_element_type=jnp.float32) + bk_ref[...]
+    cosf, sinf = cos_ref[...], sin_ref[...]
+    width = keys.shape[1]
+    keys = jnp.concatenate(
+        [turned(keys[:, i:i + HD], cosf, sinf) for i in range(0, width, HD)], axis=1
+    ).astype(jnp.bfloat16)
+    values = (jnp.dot(x, wv_ref[...], preferred_element_type=jnp.float32) + bv_ref[...]).astype(
+        jnp.bfloat16
+    )
+    k_ref[...] = keys
+    v_ref[...] = values
+
+    @pl.when(j == 0)
+    def _():
+        keep_ref[:, :width] = keys
+        keep_ref[:, width:] = values
+
+    @pl.when(j == 1)
+    def _():
+        send_ref[:, :width] = keys
+        send_ref[:, width:] = values
+
+
+def project_kv(scalars, own, got, gain, cosf, sinf, wk, wv, bk, bv):
+    rows, half = own.shape
+    depth, cols = wk.shape
+    width = cols // 2
+    whole = lambda shape: pl.BlockSpec(shape, lambda j, s: (0, 0))
+    side = lambda j, s: (0, lax.rem(j + s[1], 2))
+    bf = jnp.bfloat16
+    return pl.pallas_call(
+        kv_kernel,
+        out_shape=(
+            jax.ShapeDtypeStruct((rows, cols), bf),
+            jax.ShapeDtypeStruct((rows, cols), bf),
+            jax.ShapeDtypeStruct((rows, cols), bf),
+            jax.ShapeDtypeStruct((rows, cols), bf),
+            jax.ShapeDtypeStruct((rows, depth), bf),
+        ),
+        grid_spec=pltpu.PrefetchScalarGridSpec(
+            num_scalar_prefetch=1,
+            grid=(2,),
+            in_specs=[
+                whole((rows, half)), whole((rows, half)), whole((1, depth)),
+                whole((rows, HD)), whole((rows, HD)),
+                pl.BlockSpec((depth, width), side), pl.BlockSpec((depth, width), side),
+                pl.BlockSpec((1, width), side), pl.BlockSpec((1, width), side),
+            ],
+            out_specs=[
+                pl.BlockSpec((rows, width), side), pl.BlockSpec((rows, width), side),
+                whole((rows, cols)), whole((rows, cols)), whole((rows, depth)),
+            ],
+        ),
+        cost_estimate=pl.CostEstimate(
+            flops=4 * rows * depth * cols, transcendentals=0, bytes_accessed=4 * depth * cols
+        ),
+        name="project_kv",
+    )(scalars, own, got, gain, cosf, sinf, wk, wv, bk, bv)
+
+
+def q_kernel(steps, s_ref, *refs):
+    x_refs = refs[:CHUNKS]
+    cos_ref, sin_ref, w_ref, b_ref, keep_ref, send_ref = refs[CHUNKS:]
+    j = pl.program_id(0)
+    rows = x_refs[0].shape[0]
+    outs = []
+    for t, x_ref in enumerate(x_refs):
+        q = jnp.dot(x_ref[...], w_ref[...], preferred_element_type=jnp.float32) + b_ref[...]
+        cosf = cos_ref[t * rows:(t + 1) * rows, :]
+        sinf = sin_ref[t * rows:(t + 1) * rows, :]
+        outs.append(jnp.concatenate(
+            [turned(q[:, i:i + HD], cosf, sinf) for i in range(0, q.shape[1], HD)], axis=1
+        ).astype(jnp.bfloat16))
+
+    @pl.when(j < steps)
+    def _():
+        for t, out in enumerate(outs):
+            keep_ref[t * rows:(t + 1) * rows, :] = out
+
+    @pl.when(j >= steps)
+    def _():
+        for t, out in enumerate(outs):
+            send_ref[t * rows:(t + 1) * rows, :] = out
+
+
+def project_q(scalars, normed, cosf, sinf, wq, bq):
+    rows, depth = normed[0].shape
+    tokens = rows * len(normed)
+    cols = wq.shape[1]
+    width = math.gcd(cols // 2, 2 * HD)
+    steps = cols // 2 // width
+    whole = lambda shape: pl.BlockSpec(shape, lambda j, s: (0, 0))
+    side = lambda j, s: (0, lax.rem(j // steps + s[1], 2) * steps + lax.rem(j, steps))
+    return pl.pallas_call(
+        functools.partial(q_kernel, steps),
+        out_shape=(jax.ShapeDtypeStruct((tokens, cols // 2), jnp.bfloat16),) * 2,
+        grid_spec=pltpu.PrefetchScalarGridSpec(
+            num_scalar_prefetch=1,
+            grid=(2 * steps,),
+            in_specs=[whole((rows, depth))] * len(normed) + [
+                whole((tokens, HD)), whole((tokens, HD)),
+                pl.BlockSpec((depth, width), side), pl.BlockSpec((1, width), side),
+            ],
+            out_specs=[
+                pl.BlockSpec((tokens, width), lambda j, s: (0, jnp.minimum(j, steps - 1))),
+                pl.BlockSpec((tokens, width), lambda j, s: (0, jnp.maximum(j - steps, 0))),
+            ],
+        ),
+        cost_estimate=pl.CostEstimate(
+            flops=2 * tokens * depth * cols, transcendentals=0, bytes_accessed=2 * depth * cols
+        ),
+        name="project_q",
+    )(scalars, *normed, cosf, sinf, wq, bq)
+
+
+def attend_kernel(units, heads, group, first, last, t_ref, *refs):
+    q_refs, refs = refs[:2], refs[2:]
+    pos_ref, low_ref, refs = refs[0], refs[1], refs[2:]
+    u_refs, refs = refs[:units], refs[units:]
+    if not first:
+        (m_in, l_in, acc_in), refs = refs[:3], refs[3:]
+    if last:
+        out_refs, refs = refs[:2], refs[2:]
+        m_ref, l_ref, acc_ref, kv, q_all = refs
+    else:
+        m_ref, l_ref, acc_ref, kv, q_all = refs
+    keys = u_refs[0].shape[0]
+    rows = q_refs[0].shape[0]
+    tiles = 2 * heads * group
+    if first:
+        m_ref[...] = jnp.full(m_ref.shape, NEG, jnp.float32)
+        l_ref[...] = jnp.zeros(l_ref.shape, jnp.float32)
+        acc_ref[...] = jnp.zeros(acc_ref.shape, jnp.float32)
+    else:
+        m_ref[...] = m_in[...]
+        l_ref[...] = l_in[...]
+        acc_ref[...] = acc_in[...]
+    for n in range(units):
+        kv[n] = u_refs[n][...]
+    for half in range(2):
+        for g in range(heads * group):
+            q_all[half * heads * group + g] = q_refs[half][:, g * HD:(g + 1) * HD]
+    factor = HD ** (-0.5) * math.log2(math.e)
+
+    def step(n, masked):
+        def tile(i, carry):
+            half = i // (heads * group)
+            head = lax.rem(i, heads * group) // group
+            k = kv[n, :, pl.ds(pl.multiple_of(head * HD, HD), HD)]
+            v = kv[n, :, pl.ds(pl.multiple_of((heads + head) * HD, HD), HD)]
+            s = lax.dot_general(
+                k, q_all[i], (((1,), (1,)), ((), ())), preferred_element_type=jnp.float32
+            )
+            old = m_ref[i]
+            if masked:
+                at = lax.broadcasted_iota(jnp.int32, (keys, 1), 0)
+                at = at + jnp.where(at < keys // 2, t_ref[n, 1], t_ref[n, 2] - keys // 2)
+                allowed = (at >= low_ref[half]) & (at <= pos_ref[half])
+                s = jnp.where(allowed, s, NEG)
+            new = jnp.maximum(old, jnp.max(s, axis=0, keepdims=True))
+            p = jnp.exp2((s - new) * factor)
+            if masked:
+                p = jnp.where(allowed, p, 0.0)
+            alpha = jnp.exp2((old - new) * factor)
+            m_ref[i] = new
+            l_ref[i] = l_ref[i] * alpha + jnp.sum(p, axis=0, keepdims=True)
+            added = lax.dot_general(
+                v, p.astype(jnp.bfloat16), (((0,), (0,)), ((), ())),
+                preferred_element_type=jnp.float32,
+            )
+            acc_ref[i] = acc_ref[i] * alpha + added
+            return carry
+
+        lax.fori_loop(0, tiles, tile, 0)
+
+    def unit(n, carry):
+        state = t_ref[n, 0]
+
+        @pl.when(state == 1)
+        def _():
+            step(n, False)
+
+        @pl.when(state == 2)
+        def _():
+            step(n, True)
+
+        return carry
+
+    lax.fori_loop(0, units, unit, 0)
+    if last:
+        for half in range(2):
+            for g in range(heads * group):
+                i = half * heads * group + g
+                out_refs[half][:, g * HD:(g + 1) * HD] = (acc_ref[i] / l_ref[i]).T.astype(
+                    jnp.bfloat16
+                )
+
+
+def attend(table, queries, pos, low, units, state, heads, group, last, name):
+    rows, cols = queries[0].shape
+    keys = units[0].shape[0]
+    tiles = 2 * heads * group
+    first = state is None
+    vm = pl.BlockSpec(memory_space=pltpu.VMEM)
+    stat = jax.ShapeDtypeStruct((tiles, 1, rows), jnp.float32)
+    accs = jax.ShapeDtypeStruct((tiles, HD, rows), jnp.float32)
+    scratch = [
+        pltpu.VMEM((len(units), keys, units[0].shape[1]), jnp.bfloat16),
+        pltpu.VMEM((tiles, rows, HD), jnp.bfloat16),
+    ]
+    if last:
+        out_shape = (jax.ShapeDtypeStruct((rows, cols), jnp.bfloat16),) * 2
+        scratch = [
+            pltpu.VMEM(stat.shape, jnp.float32), pltpu.VMEM(stat.shape, jnp.float32),
+            pltpu.VMEM(accs.shape, jnp.float32),
+        ] + scratch
+    else:
+        out_shape = (stat, stat, accs)
+    args = [*queries, pos, low, *units] + ([] if first else list(state))
+    return pl.pallas_call(
+        functools.partial(attend_kernel, len(units), heads, group, first, last),
+        out_shape=out_shape,
+        in_specs=[pl.BlockSpec(memory_space=pltpu.SMEM)] + [vm] * len(args),
+        out_specs=[vm] * len(out_shape),
+        scratch_shapes=scratch,
+        cost_estimate=pl.CostEstimate(
+            flops=4 * tiles * rows * keys * HD * len(units),
+            transcendentals=tiles * rows * keys * len(units),
+            bytes_accessed=4 * tiles * rows * HD,
+        ),
+        name=name,
+    )(table, *args)
+
+
+def out_kernel(s_ref, h_ref, *refs):
+    a_refs, (w_ref, out_ref) = refs[:4], refs[4:]
+    depth = a_refs[0].shape[1]
+    total = h_ref[...].astype(jnp.float32)
+    for n, a_ref in enumerate(a_refs):
+        rows = pl.ds(pl.multiple_of(s_ref[2 + n] * depth, depth), depth)
+        total = total + jnp.dot(a_ref[...], w_ref[rows, :], preferred_element_type=jnp.float32)
+    out_ref[...] = total.astype(out_ref.dtype)
+
+
+def project_out(scalars, hidden, pieces, w_out):
+    rows, cols = hidden.shape
+    depth = w_out.shape[0]
+    width = math.gcd(cols, 512)
+    whole = lambda a: pl.BlockSpec(a.shape, lambda j, s: (0, 0))
+    return pl.pallas_call(
+        out_kernel,
+        out_shape=jax.ShapeDtypeStruct((rows, cols), jnp.bfloat16),
+        grid_spec=pltpu.PrefetchScalarGridSpec(
+            num_scalar_prefetch=1,
+            grid=(cols // width,),
+            in_specs=[pl.BlockSpec((rows, width), lambda j, s: (0, j))]
+            + [whole(a) for a in pieces]
+            + [pl.BlockSpec((depth, width), lambda j, s: (0, j))],
+            out_specs=pl.BlockSpec((rows, width), lambda j, s: (0, j)),
+        ),
+        cost_estimate=pl.CostEstimate(
+            flops=2 * rows * depth * cols, transcendentals=0, bytes_accessed=2 * depth * cols
+        ),
+        name="project_out",
+    )(scalars, hidden, *pieces, w_out)
+
+
+def local(
+    planes, hidden_in, norm_gain, seq_lengths, w_query, b_query, w_key, b_key, w_value, b_value,
+    w_out,
+):
+    rows, half = hidden_in.shape
+    part = rows // CHUNKS
+    heads = w_key.shape[1] // HD // 2
+    group = w_query.shape[1] // w_key.shape[1]
+    tp = lax.axis_index("tp")
+    cp = lax.axis_index("cp")
+    core, row, plane = cp % 2, cp // 2 % 2, cp // 4
+    chip = cp // 2
+    f32 = jnp.float32
+
+    def pairs(move):
+        found = []
+        for z in range(planes):
+            for y in range(2):
+                for c in range(2):
+                    for x in range(2):
+                        to = move(z, y, c, x)
+                        if to is not None:
+                            found.append((
+                                ((z * 2 + y) * 2 + c) * 2 + x,
+                                ((to[0] * 2 + to[1]) * 2 + to[2]) * 2 + to[3],
+                            ))
+        return found
+
+    over_x = pairs(lambda z, y, c, x: (z, y, c, 1 - x))
+    over_c = pairs(lambda z, y, c, x: (z, y, 1 - c, x))
+    over_xc = pairs(lambda z, y, c, x: (z, y, 1 - c, 1 - x))
+
+    def up(k):
+        return pairs(lambda z, y, c, x: (z + 1, y, c, x) if k <= z + 1 < planes else None)
+
+    def across(k):
+        return pairs(
+            lambda z, y, c, x: (z, 1 - y, c, x) if z >= k and (k > 0 or y == 0) else None
+        )
+
+    def send(a, route):
+        return lax.ppermute(a, SIZES, route)
+
+    chunks = [hidden_in[t * part:(t + 1) * part] for t in range(CHUNKS)]
+    got = [send(a, over_x) for a in chunks]
+
+    ends = jnp.cumsum(seq_lengths)
+    starts = ends - seq_lengths
+    chip_pos = jnp.stack([
+        cp * rows + jnp.arange(rows, dtype=jnp.int32),
+        (cp + 1 - 2 * core) * rows + jnp.arange(rows, dtype=jnp.int32),
+    ])
+    low = jnp.max(
+        jnp.where(starts[None, None, :] <= chip_pos[..., None], starts[None, None, :], 0), axis=-1
+    )
+    local_pos = (chip_pos - low)[0]
+    freq = ROPE_BASE ** (-jnp.arange(HD // 2, dtype=f32) / (HD // 2))
+    angle = local_pos.astype(f32)[:, None] * freq[None, :]
+    cosine, sine = jnp.cos(angle), jnp.sin(angle)
+    cosf = jnp.concatenate([cosine, cosine], axis=1)
+    sinf = jnp.concatenate([-sine, sine], axis=1)
+    other = (1 - tp) * 2
+    scalars = jnp.stack(
+        [tp, core, tp * 2 + core, tp * 2 + 1 - core, other + core, other + 1 - core]
+    ).astype(jnp.int32)
+
+    span = 2 * rows
+    q_from, q_to = chip * span, chip * span + span - 1
+    low_min = jnp.min(low)
+    low_max = jnp.max(low)
+    shift = jnp.array([[k, flip, t] for k in range(planes) for flip in range(2)
+                       for t in range(CHUNKS)], jnp.int32)
+    source = (plane - shift[:, 0]) * 2 + jnp.where(shift[:, 1] == 0, row, 1 - row)
+    first_pos = source * span + core * rows + shift[:, 2] * part
+    second_pos = source * span + (1 - core) * rows + shift[:, 2] * part
+    k_from = jnp.minimum(first_pos, second_pos)
+    k_to = jnp.maximum(first_pos, second_pos) + part - 1
+    valid = (plane >= shift[:, 0]) & (k_to >= low_min) & (k_from <= q_to)
+    free = (k_from >= low_max) & (k_to <= q_from)
+    states = jnp.where(valid, jnp.where(free, 1, 2), 0)
+    table = jnp.stack([states, first_pos, second_pos], axis=1).astype(jnp.int32)
+
+    gain = norm_gain[None, :]
+    bk, bv, bq = (b.astype(f32)[None, :] for b in (b_key, b_value, b_query))
+    k_parts, v_parts, normed, units = [], [], [], [[None] * CHUNKS for _ in range(2 * planes)]
+    for t in range(CHUNKS):
+        here = slice(t * part, (t + 1) * part)
+        k, v, keep, give, norm = project_kv(
+            scalars, chunks[t], got[t], gain, cosf[here], sinf[here],
+            w_key, w_value, bk, bv,
+        )
+        k_parts.append(k)
+        v_parts.append(v)
+        normed.append(norm)
+        column = jnp.concatenate([keep, send(give, over_c)], axis=0)
+        for k in range(planes):
+            units[2 * k][t] = column
+            units[2 * k + 1][t] = send(column, across(k))
+            if k + 1 < planes:
+                column = send(column, up(k + 1))
+    q_keep, q_give = project_q(scalars, normed, cosf, sinf, w_query, bq)
+    queries = (q_keep, send(q_give, over_c))
+
+    pos, low = chip_pos[:, None, :], low[:, None, :]
+    state = None
+    for n, planes_here in enumerate(((0,), tuple(range(1, planes - 1)), (planes - 1,))):
+        if not planes_here:
+            continue
+        mine, lines = [], []
+        for k in planes_here:
+            for flip in range(2):
+                for t in range(CHUNKS):
+                    mine.append(units[2 * k + flip][t])
+                    lines.append((2 * k + flip) * CHUNKS + t)
+        state = attend(
+            table[lines[0]:lines[-1] + 1], queries, pos, low, mine, state, heads, group,
+            planes_here[-1] == planes - 1, f"attend_{n}",
+        )
+    att_own, att_partner = state
+    pieces = (att_own, send(att_partner, over_c), send(att_own, over_x), send(att_partner, over_xc))
+    mixed = project_out(scalars, hidden_in, pieces, w_out)
+    return (mixed, jnp.concatenate(k_parts, axis=0), jnp.concatenate(v_parts, axis=0))
 
 
 def solution(mesh):
@@ -147,10 +557,16 @@
         P("tp"),
         P(None, "tp"),
     )
-    return jax.shard_map(
-        local,
-        mesh=mesh,
-        in_specs=placed,
-        out_specs=(P("cp", "tp"), P("cp", "tp"), P("cp", "tp")),
-        check_vma=False,
-    )
+    out = (P("cp", "tp"), P("cp", "tp"), P("cp", "tp"))
+
+    def call(*args):
+        cp, tp = mesh.shape["cp"], mesh.shape["tp"]
+        rows = args[0].shape[0] // cp
+        kv_heads = args[5].shape[1] // tp // HD
+        fits = tp == 2 and cp % 4 == 0 and cp >= 8 and kv_heads % 2 == 0 and rows % 32 == 0
+        body = functools.partial(local, cp // 4) if fits else general
+        return jax.shard_map(
+            body, mesh=mesh, in_specs=placed, out_specs=out, check_vma=False
+        )(*args)
+
+    return call

time: 289 us -> 218 us (0.75)
  Pallas kernels: 0 us -> 124 us
  waiting for transfers between devices: 151 us -> 30 us
  matrix products: 62.7 us -> 0 us
  starting transfers between devices: 0.34 us -> 41.4 us
  other arithmetic: 24.7 us -> 8.94 us
  between operations: 14 us -> 1.26 us
  local copies, waits for them, and re-layouts: 22.8 us -> 11.1 us
  loops' own time: 11.1 us -> 0 us
    all_gather x4 -> x0, waiting for transfers between devices: 150 us -> none  [the longest x1 47.1 us: local(): lax.all_gather(value_heads, 'cp', axis=0, tiled=True)]
    pallas_call x0 -> x7, Pallas kernels: none -> 124 us  [the longest x3 84.7 us: attend(): pl.pallas_call(functools.partial(attend_kernel, len(units), heads, group,...]
    dot_general x16 -> x0, matrix products: 62.7 us -> none  [the longest x6 19.7 us: compute(): jnp.einsum('hgqk,khd->qhgd', weights.astype(jnp.bfloat16), value_block, p...]
    ppermute x0 -> x22, starting transfers between devices: none -> 41.4 us  [send(): return lax.ppermute(a, SIZES, route)]
    ppermute x0 -> x22, waiting for transfers between devices: none -> 30 us  [send(): return lax.ppermute(a, SIZES, route)]
    another operation x9 -> x0, loops' own time: 11.1 us -> none  [the longest x1 10.7 us: local(): lax.scan(advance, carried, (key_split, value_split, jnp.arange(blocks, dt...]
    reduce_sum x16 -> x0, other arithmetic: 10.9 us -> none  [the longest x6 7.77 us: compute(): totals = totals * factor + jnp.sum(weights, axis=-1)]
    reduce_or x8 -> x0, other arithmetic: 7.25 us -> none  [update(): return lax.cond(jnp.any(allowed), compute, unchanged, carried)]
  transfers between devices with their start and end apart: 4 -> 22, of which waited for: 4 -> 6; matrix products, arithmetic and copies ran while one was open for 9% -> 7% of each run, Pallas kernels for 0% -> 41%
where the time goes in v1:
time: 218 us; the launch traced here: 217 us
  Pallas kernels  124 us (57%)
  starting transfers between devices  41.4 us (19%)
  waiting for transfers between devices  30 us (14%)
  local copies, waits for them, and re-layouts  11.1 us (5%)
  other arithmetic  8.94 us (4%)
    pallas_call x3, Pallas kernels, attend(): pl.pallas_call(functools.partial(attend_kernel, len(units), heads, group,...  84.7 us
    ppermute x22, starting transfers between devices, send(): return lax.ppermute(a, SIZES, route)  41.4 us
    ppermute x22, waiting for transfers between devices, send(): return lax.ppermute(a, SIZES, route)  30 us
    pallas_call x2, Pallas kernels, project_kv(): pl.pallas_call(kv_kernel, out_shape=(jax.ShapeDtypeStruct((rows, cols), b...  16.6 us
    pallas_call x1, Pallas kernels, project_q(): pl.pallas_call(functools.partial(q_kernel, steps), out_shape=(jax.ShapeDt...  12 us
    pallas_call x1, Pallas kernels, project_out(): pl.pallas_call(out_kernel, out_shape=jax.ShapeDtypeStruct((rows, cols), j...  11 us
    unnamed x77, local copies, waits for them, and re-layouts  7.03 us
  transfers between devices with their start and end apart: 22, of which 6 were waited for; matrix products, arithmetic and copies ran while one was open for 7% of the time, Pallas kernels for 41%

profile of v1, /device:TPU:25, one launch (start us, length us, event | category | flops | bytes accessed | tf_op | source)
XLA Modules:
  0.0 216.9 jit_solution(17045932353901858410)
XLA Ops:
  0.7 1.4 fusion.10
  2.1 1.3 collective-permute-start.1
  3.9 0.7 select_reduce_fusion.1
  7.6 0.8 fusion.1
  8.4 0.7 pad_maximum_fusion.3.refs_3_
  9.1 0.7 fusion.3
  9.9 0.7 pad_maximum_fusion.2.refs_2_
  10.6 7.2 %collective-permute-done.1.got_ref = bf16[128,2560]{1,0:T(8,128)(2,1)S(1)} collective-permute-done((bf16[128,2560]{1,0:T(8,128)(2,1)S(1)}, bf16[128,2560]{1,0:T(8,128)(2,1)S(1)}, u32[]{:S(2)}, u32[]{:S(2)}) %collective-permute-start.1) | collective-permute-done | bytes 655392 | tf_op jit(solution)/shard_map/ppermute | solution.py:464
  17.8 0.8 copy-done.3
  18.6 8.2 %project_kv.3 = (bf16[128,512]{1,0:T(8,128)(2,1)}, bf16[128,512]{1,0:T(8,128)(2,1)}, bf16[128,512]{1,0:T(8,128)(2,1)}, bf16[128,512]{1,0:T(8,128)(2,1)}, bf16[128,5120]{1,0:T(8,128)(2,1)}) custom-call(s32[6]{0:T(128)} %stack.38.s_ref, bf16[128,2560]{1,0:T(8,128)(2,1)} %copy-done.1, bf16[128,2560]{1,0:T(8,128)(2,1)} %copy-done.3, f32[1,5120]{1,0:T(1,128)} %bitcast.11, ...), custom_call_target="tpu_custom_call" | custom-call | flops 1342177280 | bytes 10485760 | tf_op jit(solution)/shard_map/project_kv/pallas_call | solution.py:186
  26.9 2.7 %collective-permute-start.7 = (bf16[128,512]{1,0:T(8,128)(2,1)}, bf16[128,512]{1,0:T(8,128)(2,1)S(1)}, u32[]{:S(2)}, u32[]{:S(2)}) collective-permute-start(bf16[128,512]{1,0:T(8,128)(2,1)} %get-tuple-element.30), channel_id=1, source_target_pairs={{0,2},{1,3},{2,0},{3,1},{4,6},{5,7},{6,4},{7,5},{8,10},{9,11},{10,... | collective-permute-start | bytes 393224 | tf_op jit(solution)/shard_map/ppermute | solution.py:464
  29.6 2.2 %collective-permute-done.got_ref = bf16[128,2560]{1,0:T(8,128)(2,1)S(1)} collective-permute-done((bf16[128,2560]{1,0:T(8,128)(2,1)S(1)}, bf16[128,2560]{1,0:T(8,128)(2,1)S(1)}, u32[]{:S(2)}, u32[]{:S(2)}) %collective-permute-start) | collective-permute-done | bytes 655392 | tf_op jit(solution)/shard_map/ppermute | solution.py:464
  31.8 0.8 copy-done.2
  32.7 8.3 %project_kv.2 = (bf16[128,512]{1,0:T(8,128)(2,1)}, bf16[128,512]{1,0:T(8,128)(2,1)}, bf16[128,512]{1,0:T(8,128)(2,1)}, bf16[128,512]{1,0:T(8,128)(2,1)}, bf16[128,5120]{1,0:T(8,128)(2,1)}) custom-call(s32[6]{0:T(128)} %stack.38.s_ref, bf16[128,2560]{1,0:T(8,128)(2,1)} %copy-done, bf16[128,2560]{1,0:T(8,128)(2,1)} %copy-done.2, f32[1,5120]{1,0:T(1,128)} %bitcast.12, ...), custom_call_target="tpu_custom_call" | custom-call | flops 1342177280 | bytes 10485760 | tf_op jit(solution)/shard_map/project_kv/pallas_call | solution.py:186
  41.0 1.6 collective-permute-start.3
  42.6 0.9 constant_dynamic-update-slice_fusion.1
  43.6 3.2 %collective-permute-start.18 = (bf16[256,512]{1,0:T(8,128)(2,1)S(1)}, bf16[256,512]{1,0:T(8,128)(2,1)S(1)}, u32[]{:S(2)}, u32[]{:S(2)}) collective-permute-start(bf16[256,512]{1,0:T(8,128)(2,1)S(1)} %constant_dynamic-update-slice_fusion.2.refs_5_), channel_id=1, source_target_pairs={{0,4},{1,5},{2,6},{3,7},{8,12},{9,13},{10,14},{11,15},{16,20},{17,... | collective-permute-start | bytes 786440 | tf_op jit(solution)/shard_map/ppermute | solution.py:464
  46.8 1.3 collective-permute-start.8
  48.1 1.3 collective-permute-start.4
  49.4 12.0 %project_q.1 = (bf16[256,768]{1,0:T(8,128)(2,1)}, bf16[256,768]{1,0:T(8,128)(2,1)}) custom-call(s32[6]{0:T(128)} %stack.38.s_ref, bf16[128,5120]{1,0:T(8,128)(2,1)} %get-tuple-element.23.refs_0_, bf16[128,5120]{1,0:T(8,128)(2,1)} %get-tuple-element.24.refs_1_, f32[256,128]{1,0:T(8,128)} %pad_maximum_fusion.2.refs_2_, f32[256,128]{1,0:T(8,128)} %pad_maximum_fusion.3.refs_3_, ...), custom_call_target="tpu_custom_call" | custom-call | flops 4026531840 | bytes 15728640 | tf_op jit(solution)/shard_map/project_q/pallas_call | solution.py:249
  62.5 1.3 collective-permute-start.17
  63.8 1.3 collective-permute-start.9
  65.1 1.9 collective-permute-start.14
  67.1 1.3 collective-permute-start.5
  68.4 1.2 and_select_fusion.1
  69.7 3.6 %collective-permute-start.13 = (bf16[256,512]{1,0:T(8,128)(2,1)S(1)}, bf16[256,512]{1,0:T(8,128)(2,1)S(1)}, u32[]{:S(2)}, u32[]{:S(2)}) collective-permute-start(bf16[256,512]{1,0:T(8,128)(2,1)S(1)} %collective-permute-done.4.refs_4_), channel_id=1, source_target_pairs={{8,12},{9,13},{10,14},{11,15},{12,8},{13,9},{14,10},{15,11},{16,20... | collective-permute-start | bytes 786440 | tf_op jit(solution)/shard_map/ppermute | solution.py:464
  73.3 1.8 collective-permute-done.9.refs_9_
  75.2 1.9 collective-permute-start.16
  77.1 1.3 collective-permute-start.10
  78.4 2.4 %collective-permute-done.5.refs_8_ = bf16[256,512]{1,0:T(8,128)(2,1)S(1)} collective-permute-done((bf16[256,512]{1,0:T(8,128)(2,1)S(1)}, bf16[256,512]{1,0:T(8,128)(2,1)S(1)}, u32[]{:S(2)}, u32[]{:S(2)}) %collective-permute-start.5) | collective-permute-done | bytes 262176 | tf_op jit(solution)/shard_map/ppermute | solution.py:464
  80.8 1.9 collective-permute-start.15
  82.7 1.3 collective-permute-start.6
  85.3 0.7 copy.35.t_ref
  86.0 0.7 copy.34.t_ref
  86.7 0.7 copy.33.t_ref
  87.3 13.6 %attend_0.1 = (f32[12,1,256]{2,1,0:T(1,128)}, f32[12,1,256]{2,1,0:T(1,128)}, f32[12,128,256]{2,1,0:T(8,128)}) custom-call(s32[4,3]{1,0:T(4,128)} %copy.35.t_ref, bf16[256,768]{1,0:T(8,128)(2,1)} %get-tuple-element.25.refs_0_, bf16[256,768]{1,0:T(8,128)(2,1)} %copy-done.22, s32[2,1,256]{2,1,0:T(1,128)} %broadcast_in_dim.63.refs_2_, ...), custom_call_target="tpu_custom_call" | custom-call | flops 1610612736 | bytes 1572864 | tf_op jit(solution)/shard_map/attend_0/pallas_call | solution.py:375
  100.9 8.7 %collective-permute-start.12 = (bf16[256,512]{1,0:T(8,128)(2,1)S(1)}, bf16[256,512]{1,0:T(8,128)(2,1)S(1)}, u32[]{:S(2)}, u32[]{:S(2)}) collective-permute-start(bf16[256,512]{1,0:T(8,128)(2,1)S(1)} %collective-permute-done.10.refs_5_), channel_id=1, source_target_pairs={{24,28},{25,29},{26,30},{27,31},{28,24},{29,25},{30,26},{31,27}} | collective-permute-start | bytes 786440 | tf_op jit(solution)/shard_map/ppermute | solution.py:464
  109.6 1.9 collective-permute-start.11
  112.4 46.4 %attend_1.1 = (f32[12,1,256]{2,1,0:T(1,128)}, f32[12,1,256]{2,1,0:T(1,128)}, f32[12,128,256]{2,1,0:T(8,128)}) custom-call(s32[8,3]{1,0:T(8,128)} %copy.34.t_ref, bf16[256,768]{1,0:T(8,128)(2,1)} %get-tuple-element.25.refs_0_, bf16[256,768]{1,0:T(8,128)(2,1)} %copy-done.22, s32[2,1,256]{2,1,0:T(1,128)} %broadcast_in_dim.63.refs_2_, ...), custom_call_target="tpu_custom_call" | custom-call | flops 3221225472 | bytes 1572864 | tf_op jit(solution)/shard_map/attend_1/pallas_call | solution.py:375
  159.6 24.7 %attend_2.1 = (bf16[256,768]{1,0:T(8,128)(2,1)}, bf16[256,768]{1,0:T(8,128)(2,1)}) custom-call(s32[4,3]{1,0:T(4,128)} %copy.33.t_ref, bf16[256,768]{1,0:T(8,128)(2,1)} %get-tuple-element.25.refs_0_, bf16[256,768]{1,0:T(8,128)(2,1)} %copy-done.22, s32[2,1,256]{2,1,0:T(1,128)} %broadcast_in_dim.63.refs_2_, s32[2,1,256]{2,1,0:T(1,128)} %broadcast_in_dim.64.refs_3_, ...), custom_call_target="tpu_custom_call" | custom-call | flops 1610612736 | bytes 1572864 | tf_op jit(solution)/shard_map/attend_2/pallas_call | solution.py:375
  184.4 1.3 collective-permute-start.19
  185.7 1.2 collective-permute-start.20
  187.4 0.7 pad_maximum_fusion
  188.1 0.7 pad_maximum_fusion.1
  188.8 7.7 %collective-permute-done.20.refs_2_ = bf16[256,768]{1,0:T(8,128)(2,1)S(1)} collective-permute-done((bf16[256,768]{1,0:T(8,128)(2,1)}, bf16[256,768]{1,0:T(8,128)(2,1)S(1)}, u32[]{:S(2)}, u32[]{:S(2)}) %collective-permute-start.20) | collective-permute-done | bytes 393248 | tf_op jit(solution)/shard_map/ppermute | solution.py:464
  196.5 8.6 %collective-permute-done.21.refs_3_ = bf16[256,768]{1,0:T(8,128)(2,1)S(1)} collective-permute-done((bf16[256,768]{1,0:T(8,128)(2,1)}, bf16[256,768]{1,0:T(8,128)(2,1)S(1)}, u32[]{:S(2)}, u32[]{:S(2)}) %collective-permute-start.21) | collective-permute-done | bytes 393248 | tf_op jit(solution)/shard_map/ppermute | solution.py:464
  205.2 0.7 copy-done.6
  205.9 11.0 %project_out.1 = bf16[256,2560]{1,0:T(8,128)(2,1)} custom-call(s32[6]{0:T(128)} %stack.38.s_ref, bf16[256,2560]{1,0:T(8,128)(2,1)} %h_ref.1, bf16[256,768]{1,0:T(8,128)(2,1)} %get-tuple-element.37.refs_0_, bf16[256,768]{1,0:T(8,128)(2,1)} %copy-done.4, bf16[256,768]{1,0:T(8,128)(2,1)} %copy-done.5, bf16[256,768]{1,0:T(8,128)(2,1)} %copy-done.6, ...), custom_call_target="tpu_custom_call" | custom-call | flops 4026531840 | bytes 15728640 | tf_op jit(solution)/shard_map/project_out/pallas_call | solution.py:405
  (110 shorter events, 8.0 us)
Async XLA Ops:
  0.7 5.7 %copy-start.14 = (bf16[1536]{0:T(1024)(128)(2,1)S(1)}, bf16[1536]{0:T(1024)(128)(2,1)}, u32[]{:S(2)}) copy-start(bf16[1536]{0:T(1024)(128)(2,1)} %param.15) | copy-start | bytes 9220
  2.1 15.7 %copy-start.1 = (bf16[128,2560]{1,0:T(8,128)(2,1)}, bf16[128,2560]{1,0:T(8,128)(2,1)S(1)}, u32[]{:S(2)}) copy-start(bf16[128,2560]{1,0:T(8,128)(2,1)S(1)} %get-tuple-element.48.own_ref) | copy-start | bytes 1966084
  2.1 24.8 %copy-start = (bf16[128,2560]{1,0:T(8,128)(2,1)}, bf16[128,2560]{1,0:T(8,128)(2,1)S(1)}, u32[]{:S(2)}) copy-start(bf16[128,2560]{1,0:T(8,128)(2,1)S(1)} %get-tuple-element.49.own_ref) | copy-start | bytes 1966084
  2.1 15.7 %collective-permute-start.1 = (bf16[128,2560]{1,0:T(8,128)(2,1)S(1)}, bf16[128,2560]{1,0:T(8,128)(2,1)S(1)}, u32[]{:S(2)}, u32[]{:S(2)}) collective-permute-start(bf16[128,2560]{1,0:T(8,128)(2,1)S(1)} %get-tuple-element.48.own_ref), channel_id=1, source_target_pairs={{0,1},{1,0},{2,3},{3,2},{4,5},{5,4},{6,7},{7,6},{8,9},{9,8},{10,11... | collective-permute-start | bytes 1966088 | tf_op jit(solution)/shard_map/ppermute | solution.py:464
  3.4 28.4 %collective-permute-start = (bf16[128,2560]{1,0:T(8,128)(2,1)S(1)}, bf16[128,2560]{1,0:T(8,128)(2,1)S(1)}, u32[]{:S(2)}, u32[]{:S(2)}) collective-permute-start(bf16[128,2560]{1,0:T(8,128)(2,1)S(1)} %get-tuple-element.49.own_ref), channel_id=1, source_target_pairs={{0,1},{1,0},{2,3},{3,2},{4,5},{5,4},{6,7},{7,6},{8,9},{9,8},{10,11... | collective-permute-start | bytes 1966088 | tf_op jit(solution)/shard_map/ppermute | solution.py:464
  26.9 16.7 %collective-permute-start.7 = (bf16[128,512]{1,0:T(8,128)(2,1)}, bf16[128,512]{1,0:T(8,128)(2,1)S(1)}, u32[]{:S(2)}, u32[]{:S(2)}) collective-permute-start(bf16[128,512]{1,0:T(8,128)(2,1)} %get-tuple-element.30), channel_id=1, source_target_pairs={{0,2},{1,3},{2,0},{3,1},{4,6},{5,7},{6,4},{7,5},{8,10},{9,11},{10,... | collective-permute-start | bytes 393224 | tf_op jit(solution)/shard_map/ppermute | solution.py:464
  32.7 8.3 %copy-start.7 = (bf16[128,512]{1,0:T(8,128)(2,1)S(1)}, bf16[128,512]{1,0:T(8,128)(2,1)}, u32[]{:S(2)}) copy-start(bf16[128,512]{1,0:T(8,128)(2,1)} %get-tuple-element.29) | copy-start | bytes 393220
  41.0 7.0 %collective-permute-start.3 = (bf16[128,512]{1,0:T(8,128)(2,1)}, bf16[128,512]{1,0:T(8,128)(2,1)S(1)}, u32[]{:S(2)}, u32[]{:S(2)}) collective-permute-start(bf16[128,512]{1,0:T(8,128)(2,1)} %get-tuple-element.28), channel_id=1, source_target_pairs={{0,2},{1,3},{2,0},{3,1},{4,6},{5,7},{6,4},{7,5},{8,10},{9,11},{10,... | collective-permute-start | bytes 393224 | tf_op jit(solution)/shard_map/ppermute | solution.py:464
  43.6 17.9 %copy-start.13 = (bf16[256,512]{1,0:T(8,128)(2,1)}, bf16[256,512]{1,0:T(8,128)(2,1)S(1)}, u32[]{:S(2)}) copy-start(bf16[256,512]{1,0:T(8,128)(2,1)S(1)} %constant_dynamic-update-slice_fusion.2.refs_5_) | copy-start | bytes 786436
  43.6 21.5 %collective-permute-start.18 = (bf16[256,512]{1,0:T(8,128)(2,1)S(1)}, bf16[256,512]{1,0:T(8,128)(2,1)S(1)}, u32[]{:S(2)}, u32[]{:S(2)}) collective-permute-start(bf16[256,512]{1,0:T(8,128)(2,1)S(1)} %constant_dynamic-update-slice_fusion.2.refs_5_), channel_id=1, source_target_pairs={{0,4},{1,5},{2,6},{3,7},{8,12},{9,13},{10,14},{11,15},{16,20},{17,... | collective-permute-start | bytes 786440 | tf_op jit(solution)/shard_map/ppermute | solution.py:464
  46.8 17.0 %collective-permute-start.8 = (bf16[256,512]{1,0:T(8,128)(2,1)S(1)}, bf16[256,512]{1,0:T(8,128)(2,1)S(1)}, u32[]{:S(2)}, u32[]{:S(2)}) collective-permute-start(bf16[256,512]{1,0:T(8,128)(2,1)S(1)} %constant_dynamic-update-slice_fusion.2.refs_5_), channel_id=1, source_target_pairs={{0,8},{1,9},{2,10},{3,11},{4,12},{5,13},{6,14},{7,15},{8,16},{9,17... | collective-permute-start | bytes 786440 | tf_op jit(solution)/shard_map/ppermute | solution.py:464
  48.1 14.4 %copy-start.12 = (bf16[256,512]{1,0:T(8,128)(2,1)}, bf16[256,512]{1,0:T(8,128)(2,1)S(1)}, u32[]{:S(2)}) copy-start(bf16[256,512]{1,0:T(8,128)(2,1)S(1)} %constant_dynamic-update-slice_fusion.refs_4_) | copy-start | bytes 786436
  48.1 18.9 %collective-permute-start.4 = (bf16[256,512]{1,0:T(8,128)(2,1)S(1)}, bf16[256,512]{1,0:T(8,128)(2,1)S(1)}, u32[]{:S(2)}, u32[]{:S(2)}) collective-permute-start(bf16[256,512]{1,0:T(8,128)(2,1)S(1)} %constant_dynamic-update-slice_fusion.refs_4_), channel_id=1, source_target_pairs={{0,8},{1,9},{2,10},{3,11},{4,12},{5,13},{6,14},{7,15},{8,16},{9,17... | collective-permute-start | bytes 786440 | tf_op jit(solution)/shard_map/ppermute | solution.py:464
  49.4 19.0 %copy-start.18 = (s32[16,1]{0,1:T(1,128)S(1)}, s32[16,1]{0,1:T(1,128)}, u32[]{:S(2)}) copy-start(s32[16,1]{0,1:T(1,128)} %constant.81) | copy-start | bytes 196
  49.4 19.0 %copy-start.19 = (pred[16,1]{0,1:T(4,128)(4,1)S(1)}, pred[16,1]{0,1:T(4,128)(4,1)}, u32[]{:S(2)}) copy-start(pred[16,1]{0,1:T(4,128)(4,1)} %constant.83) | copy-start | bytes 52
  49.4 19.0 %copy-start.20 = (s32[16,1]{0,1:T(1,128)S(1)}, s32[16,1]{0,1:T(1,128)}, u32[]{:S(2)}) copy-start(s32[16,1]{0,1:T(1,128)} %constant.85) | copy-start | bytes 196
  49.4 18.9 %copy-start.21 = (s32[16,1]{0,1:T(1,128)S(1)}, s32[16,1]{0,1:T(1,128)}, u32[]{:S(2)}) copy-start(s32[16,1]{0,1:T(1,128)} %constant.86) | copy-start | bytes 196
  61.5 15.6 %collective-permute-start.2 = (bf16[256,768]{1,0:T(8,128)(2,1)}, bf16[256,768]{1,0:T(8,128)(2,1)S(1)}, u32[]{:S(2)}, u32[]{:S(2)}) collective-permute-start(bf16[256,768]{1,0:T(8,128)(2,1)} %get-tuple-element.26), channel_id=1, source_target_pairs={{0,2},{1,3},{2,0},{3,1},{4,6},{5,7},{6,4},{7,5},{8,10},{9,11},{10,... | collective-permute-start | bytes 1179656 | tf_op jit(solution)/shard_map/ppermute | solution.py:464
  62.5 7.2 %collective-permute-start.17 = (bf16[256,512]{1,0:T(8,128)(2,1)S(1)}, bf16[256,512]{1,0:T(8,128)(2,1)S(1)}, u32[]{:S(2)}, u32[]{:S(2)}) collective-permute-start(bf16[256,512]{1,0:T(8,128)(2,1)S(1)} %constant_dynamic-update-slice_fusion.refs_4_), channel_id=1, source_target_pairs={{0,4},{1,5},{2,6},{3,7},{8,12},{9,13},{10,14},{11,15},{16,20},{17,... | collective-permute-start | bytes 786440 | tf_op jit(solution)/shard_map/ppermute | solution.py:464
  63.8 47.8 %copy-start.23 = (bf16[256,512]{1,0:T(8,128)(2,1)}, bf16[256,512]{1,0:T(8,128)(2,1)S(1)}, u32[]{:S(2)}) copy-start(bf16[256,512]{1,0:T(8,128)(2,1)S(1)} %collective-permute-done.8.refs_5_) | copy-start | bytes 786436
  63.8 11.4 %collective-permute-start.9 = (bf16[256,512]{1,0:T(8,128)(2,1)S(1)}, bf16[256,512]{1,0:T(8,128)(2,1)S(1)}, u32[]{:S(2)}, u32[]{:S(2)}) collective-permute-start(bf16[256,512]{1,0:T(8,128)(2,1)S(1)} %collective-permute-done.8.refs_5_), channel_id=1, source_target_pairs={{8,16},{9,17},{10,18},{11,19},{12,20},{13,21},{14,22},{15,23},{16,... | collective-permute-start | bytes 786440 | tf_op jit(solution)/shard_map/ppermute | solution.py:464
  65.1 22.2 %copy-start.25 = (bf16[256,512]{1,0:T(8,128)(2,1)}, bf16[256,512]{1,0:T(8,128)(2,1)S(1)}, u32[]{:S(2)}) copy-start(bf16[256,512]{1,0:T(8,128)(2,1)S(1)} %collective-permute-done.18.refs_7_) | copy-start | bytes 786436
  65.1 17.6 %collective-permute-start.14 = (bf16[256,512]{1,0:T(8,128)(2,1)S(1)}, bf16[256,512]{1,0:T(8,128)(2,1)S(1)}, u32[]{:S(2)}, u32[]{:S(2)}) collective-permute-start(bf16[256,512]{1,0:T(8,128)(2,1)S(1)} %collective-permute-done.8.refs_5_), channel_id=1, source_target_pairs={{8,12},{9,13},{10,14},{11,15},{12,8},{13,9},{14,10},{15,11},{16,20... | collective-permute-start | bytes 786440 | tf_op jit(solution)/shard_map/ppermute | solution.py:464
  67.0 44.6 %copy-start.24 = (bf16[256,512]{1,0:T(8,128)(2,1)}, bf16[256,512]{1,0:T(8,128)(2,1)S(1)}, u32[]{:S(2)}) copy-start(bf16[256,512]{1,0:T(8,128)(2,1)S(1)} %collective-permute-done.4.refs_4_) | copy-start | bytes 786436
  67.1 13.7 %collective-permute-start.5 = (bf16[256,512]{1,0:T(8,128)(2,1)S(1)}, bf16[256,512]{1,0:T(8,128)(2,1)S(1)}, u32[]{:S(2)}, u32[]{:S(2)}) collective-permute-start(bf16[256,512]{1,0:T(8,128)(2,1)S(1)} %collective-permute-done.4.refs_4_), channel_id=1, source_target_pairs={{8,16},{9,17},{10,18},{11,19},{12,20},{13,21},{14,22},{15,23},{16,... | collective-permute-start | bytes 786440 | tf_op jit(solution)/shard_map/ppermute | solution.py:464
  69.7 17.7 %copy-start.29 = (bf16[256,512]{1,0:T(8,128)(2,1)}, bf16[256,512]{1,0:T(8,128)(2,1)S(1)}, u32[]{:S(2)}) copy-start(bf16[256,512]{1,0:T(8,128)(2,1)S(1)} %collective-permute-done.17.refs_6_) | copy-start | bytes 786436
  69.7 41.9 %collective-permute-start.13 = (bf16[256,512]{1,0:T(8,128)(2,1)S(1)}, bf16[256,512]{1,0:T(8,128)(2,1)S(1)}, u32[]{:S(2)}, u32[]{:S(2)}) collective-permute-start(bf16[256,512]{1,0:T(8,128)(2,1)S(1)} %collective-permute-done.4.refs_4_), channel_id=1, source_target_pairs={{8,12},{9,13},{10,14},{11,15},{12,8},{13,9},{14,10},{15,11},{16,20... | collective-permute-start | bytes 786440 | tf_op jit(solution)/shard_map/ppermute | solution.py:464
  75.1 36.5 %copy-start.26 = (bf16[256,512]{1,0:T(8,128)(2,1)}, bf16[256,512]{1,0:T(8,128)(2,1)S(1)}, u32[]{:S(2)}) copy-start(bf16[256,512]{1,0:T(8,128)(2,1)S(1)} %collective-permute-done.9.refs_9_) | copy-start | bytes 786436
  75.2 36.4 %collective-permute-start.16 = (bf16[256,512]{1,0:T(8,128)(2,1)S(1)}, bf16[256,512]{1,0:T(8,128)(2,1)S(1)}, u32[]{:S(2)}, u32[]{:S(2)}) collective-permute-start(bf16[256,512]{1,0:T(8,128)(2,1)S(1)} %collective-permute-done.9.refs_9_), channel_id=1, source_target_pairs={{16,20},{17,21},{18,22},{19,23},{20,16},{21,17},{22,18},{23,19},{2... | collective-permute-start | bytes 786440 | tf_op jit(solution)/shard_map/ppermute | solution.py:464
  77.1 10.3 %copy-start.22 = (bf16[256,768]{1,0:T(8,128)(2,1)}, bf16[256,768]{1,0:T(8,128)(2,1)S(1)}, u32[]{:S(2)}) copy-start(bf16[256,768]{1,0:T(8,128)(2,1)S(1)} %collective-permute-done.2.refs_1_) | copy-start | bytes 1179652
  77.1 23.8 %collective-permute-start.10 = (bf16[256,512]{1,0:T(8,128)(2,1)S(1)}, bf16[256,512]{1,0:T(8,128)(2,1)S(1)}, u32[]{:S(2)}, u32[]{:S(2)}) collective-permute-start(bf16[256,512]{1,0:T(8,128)(2,1)S(1)} %collective-permute-done.9.refs_9_), channel_id=1, source_target_pairs={{16,24},{17,25},{18,26},{19,27},{20,28},{21,29},{22,30},{23,31}} | collective-permute-start | bytes 786440 | tf_op jit(solution)/shard_map/ppermute | solution.py:464
  80.8 20.1 %copy-start.28 = (bf16[256,512]{1,0:T(8,128)(2,1)}, bf16[256,512]{1,0:T(8,128)(2,1)S(1)}, u32[]{:S(2)}) copy-start(bf16[256,512]{1,0:T(8,128)(2,1)S(1)} %collective-permute-done.5.refs_8_) | copy-start | bytes 786436
  80.8 30.8 %collective-permute-start.15 = (bf16[256,512]{1,0:T(8,128)(2,1)S(1)}, bf16[256,512]{1,0:T(8,128)(2,1)}, u32[]{:S(2)}, u32[]{:S(2)}) collective-permute-start(bf16[256,512]{1,0:T(8,128)(2,1)S(1)} %collective-permute-done.5.refs_8_), channel_id=1, source_target_pairs={{16,20},{17,21},{18,22},{19,23},{20,16},{21,17},{22,18},{23,19},{2... | collective-permute-start | bytes 786440 | tf_op jit(solution)/shard_map/ppermute | solution.py:464
  82.7 18.2 %copy-start.27 = (bf16[256,512]{1,0:T(8,128)(2,1)}, bf16[256,512]{1,0:T(8,128)(2,1)S(1)}, u32[]{:S(2)}) copy-start(bf16[256,512]{1,0:T(8,128)(2,1)S(1)} %collective-permute-done.14.refs_7_) | copy-start | bytes 786436
  82.7 26.9 %collective-permute-start.6 = (bf16[256,512]{1,0:T(8,128)(2,1)S(1)}, bf16[256,512]{1,0:T(8,128)(2,1)S(1)}, u32[]{:S(2)}, u32[]{:S(2)}) collective-permute-start(bf16[256,512]{1,0:T(8,128)(2,1)S(1)} %collective-permute-done.5.refs_8_), channel_id=1, source_target_pairs={{16,24},{17,25},{18,26},{19,27},{20,28},{21,29},{22,30},{23,31}} | collective-permute-start | bytes 786440 | tf_op jit(solution)/shard_map/ppermute | solution.py:464
  100.9 57.9 %copy-start.30 = (bf16[256,512]{1,0:T(8,128)(2,1)}, bf16[256,512]{1,0:T(8,128)(2,1)S(1)}, u32[]{:S(2)}) copy-start(bf16[256,512]{1,0:T(8,128)(2,1)S(1)} %collective-permute-done.10.refs_5_) | copy-start | bytes 786436
  100.9 57.9 %collective-permute-start.12 = (bf16[256,512]{1,0:T(8,128)(2,1)S(1)}, bf16[256,512]{1,0:T(8,128)(2,1)S(1)}, u32[]{:S(2)}, u32[]{:S(2)}) collective-permute-start(bf16[256,512]{1,0:T(8,128)(2,1)S(1)} %collective-permute-done.10.refs_5_), channel_id=1, source_target_pairs={{24,28},{25,29},{26,30},{27,31},{28,24},{29,25},{30,26},{31,27}} | collective-permute-start | bytes 786440 | tf_op jit(solution)/shard_map/ppermute | solution.py:464
  109.6 49.2 %copy-start.33 = (bf16[256,512]{1,0:T(8,128)(2,1)}, bf16[256,512]{1,0:T(8,128)(2,1)S(1)}, u32[]{:S(2)}) copy-start(bf16[256,512]{1,0:T(8,128)(2,1)S(1)} %collective-permute-done.6.refs_4_) | copy-start | bytes 786436
  109.6 49.2 %collective-permute-start.11 = (bf16[256,512]{1,0:T(8,128)(2,1)S(1)}, bf16[256,512]{1,0:T(8,128)(2,1)S(1)}, u32[]{:S(2)}, u32[]{:S(2)}) collective-permute-start(bf16[256,512]{1,0:T(8,128)(2,1)S(1)} %collective-permute-done.6.refs_4_), channel_id=1, source_target_pairs={{24,28},{25,29},{26,30},{27,31},{28,24},{29,25},{30,26},{31,27}} | collective-permute-start | bytes 786440 | tf_op jit(solution)/shard_map/ppermute | solution.py:464
  159.6 27.7 %copy-start.9 = (bf16[128,512]{1,0:T(8,128)(2,1)S(1)}, bf16[128,512]{1,0:T(8,128)(2,1)}, u32[]{:S(2)}) copy-start(bf16[128,512]{1,0:T(8,128)(2,1)} %get-tuple-element.40) | copy-start | bytes 393220
  159.6 27.7 %copy-start.11 = (bf16[128,512]{1,0:T(8,128)(2,1)S(1)}, bf16[128,512]{1,0:T(8,128)(2,1)}, u32[]{:S(2)}) copy-start(bf16[128,512]{1,0:T(8,128)(2,1)} %get-tuple-element.39) | copy-start | bytes 393220
  159.6 28.5 %copy-start.8 = (bf16[128,512]{1,0:T(8,128)(2,1)S(1)}, bf16[128,512]{1,0:T(8,128)(2,1)}, u32[]{:S(2)}) copy-start(bf16[128,512]{1,0:T(8,128)(2,1)} %get-tuple-element.42) | copy-start | bytes 393220
  159.6 28.5 %copy-start.10 = (bf16[128,512]{1,0:T(8,128)(2,1)S(1)}, bf16[128,512]{1,0:T(8,128)(2,1)}, u32[]{:S(2)}) copy-start(bf16[128,512]{1,0:T(8,128)(2,1)} %get-tuple-element.41) | copy-start | bytes 393220
  184.4 4.5 %collective-permute-start.19 = (bf16[256,768]{1,0:T(8,128)(2,1)}, bf16[256,768]{1,0:T(8,128)(2,1)S(1)}, u32[]{:S(2)}, u32[]{:S(2)}) collective-permute-start(bf16[256,768]{1,0:T(8,128)(2,1)} %get-tuple-element.38), channel_id=1, source_target_pairs={{0,2},{1,3},{2,0},{3,1},{4,6},{5,7},{6,4},{7,5},{8,10},{9,11},{10,... | collective-permute-start | bytes 1179656 | tf_op jit(solution)/shard_map/ppermute | solution.py:464
  185.7 10.9 %collective-permute-start.20 = (bf16[256,768]{1,0:T(8,128)(2,1)}, bf16[256,768]{1,0:T(8,128)(2,1)S(1)}, u32[]{:S(2)}, u32[]{:S(2)}) collective-permute-start(bf16[256,768]{1,0:T(8,128)(2,1)} %get-tuple-element.37.refs_0_), channel_id=1, source_target_pairs={{0,1},{1,0},{2,3},{3,2},{4,5},{5,4},{6,7},{7,6},{8,9},{9,8},{10,11... | collective-permute-start | bytes 1179656 | tf_op jit(solution)/shard_map/ppermute | solution.py:464
  186.9 18.3 %collective-permute-start.21 = (bf16[256,768]{1,0:T(8,128)(2,1)}, bf16[256,768]{1,0:T(8,128)(2,1)S(1)}, u32[]{:S(2)}, u32[]{:S(2)}) collective-permute-start(bf16[256,768]{1,0:T(8,128)(2,1)} %get-tuple-element.38), channel_id=1, source_target_pairs={{0,3},{1,2},{2,1},{3,0},{4,7},{5,6},{6,5},{7,4},{8,11},{9,10},{10,... | collective-permute-start | bytes 1179656 | tf_op jit(solution)/shard_map/ppermute | solution.py:464
  188.8 16.4 %copy-start.4 = (bf16[256,768]{1,0:T(8,128)(2,1)}, bf16[256,768]{1,0:T(8,128)(2,1)S(1)}, u32[]{:S(2)}) copy-start(bf16[256,768]{1,0:T(8,128)(2,1)S(1)} %collective-permute-done.19.refs_1_) | copy-start | bytes 1179652
  196.5 8.6 %copy-start.5 = (bf16[256,768]{1,0:T(8,128)(2,1)}, bf16[256,768]{1,0:T(8,128)(2,1)S(1)}, u32[]{:S(2)}) copy-start(bf16[256,768]{1,0:T(8,128)(2,1)S(1)} %collective-permute-done.20.refs_2_) | copy-start | bytes 1179652
  (10 other events, 18.1 us)
